TPU v7x, 32 devices: a whole 2x2x4 slice. The times are simulated.
32 devices in a mesh: rep: 4 (over x, core), fsdp: 8 (over z, y).
Axes of the slice: x: 2, y: 2, z: 4, core: 2. Of those that a mesh axis runs over, the one named last changes fastest.
Arguments:
- layer_inputs: bfloat16 [8192, 4608], P(('rep', 'fsdp')), may hold values from -12 to 12
- queries: bfloat16 [8192, 2048], P(('rep', 'fsdp')), may hold values from -32 to 32
- saved_keys: bfloat16 [8192, 1024], P(('rep', 'fsdp')), may hold values from -6 to 6
- saved_values: bfloat16 [8192, 1024], P(('rep', 'fsdp')), may hold values from -6 to 6
- out_grad: bfloat16 [8192, 2048], P(('rep', 'fsdp')), may hold values from -0.625 to 0.625
- global_params: float32 [4608, 1024], P('fsdp'), may hold values from -0.09375 to 0.09375
- replica_params: float32 [4, 4608, 1024], P('rep', 'fsdp'), may hold values from -0.09375 to 0.09375
- outer_momentum: float32 [4608, 1024], P('fsdp'), may hold values from -0.125 to 0.125
- next_inputs: bfloat16 [8192, 4608], P(('rep', 'fsdp')), may hold values from -6 to 6
Outputs:
- new_params: float32 [4608, 1024], P('fsdp')
- new_momentum: float32 [4608, 1024], P('fsdp')
- next_keys: bfloat16 [8192, 1024], P(('rep', 'fsdp'))
All inputs are finite; a program needn't handle non-finite values.
Results may differ from a plain program's by a relative error of at most 0.014.
Values may be sent and summed in bfloat16 or wider, within the bound.
A program may use at most 128 MiB of HBM per device.

v0:
```python
import jax
import jax.numpy as jnp
from jax import lax
from jax.sharding import PartitionSpec as P

QH = 16
KVH = 8
HD = 128


score_scale = 1.0 / 12.0
soft_cap = 50.0
rope_base = 10000.0
inner_rate = 0.02
outer_rate = 0.7
outer_beta = 0.9


def rotate_back(grads, length):
    half = grads.shape[-1] // 2
    places = jnp.arange(length).astype(jnp.float32)
    freqs = rope_base ** (-jnp.arange(half).astype(jnp.float32) / half)
    angles = (places[:, None] * freqs[None, :])[:, None, :]
    cosine = jnp.cos(angles)
    sine = jnp.sin(angles)
    first = grads[..., :half]
    second = grads[..., half:]
    return jnp.concatenate(
        [first * cosine + second * sine, second * cosine - first * sine], axis=-1
    )


def attention_keys(query_rows, key_rows, value_rows, grad_rows):
    length = query_rows.shape[0]
    group = QH // KVH
    query_wide = query_rows.reshape(length, KVH, group, HD)
    key_wide = key_rows.reshape(length, KVH, HD)
    value_wide = value_rows.reshape(length, KVH, HD)
    grad_wide = grad_rows.reshape(length, KVH, group, HD)
    logits = (
        jnp.einsum("ihgd,jhd->hgij", query_wide, key_wide, preferred_element_type=jnp.float32)
        * score_scale
    )
    capped = jnp.tanh(logits / soft_cap)
    row_index = jnp.arange(length)
    causal = row_index[:, None] >= row_index[None, :]
    unnormed = jnp.where(causal, jnp.exp(soft_cap * capped), jnp.float32(0.0))
    probs = unnormed / jnp.sum(unnormed, axis=-1, keepdims=True)
    dprobs = jnp.einsum("ihgd,jhd->hgij", grad_wide, value_wide, preferred_element_type=jnp.float32)
    center = jnp.sum(probs * dprobs, axis=-1, keepdims=True)
    dlogits = (probs * (dprobs - center) * (1.0 - capped * capped) * score_scale).astype(
        jnp.bfloat16
    )
    rotated = jnp.einsum("hgij,ihgd->jhd", dlogits, query_wide, preferred_element_type=jnp.float32)
    plain = rotate_back(rotated, length)
    return plain.reshape(length, KVH * HD).astype(jnp.bfloat16)


def body(
    layer_inputs,
    queries,
    saved_keys,
    saved_values,
    out_grad,
    global_params,
    replica_params,
    outer_momentum,
    next_inputs,
):
    key_grad = attention_keys(queries, saved_keys, saved_values, out_grad)
    replicas = lax.axis_size("rep")
    own_local = replica_params[0]
    width = key_grad.shape[1] // replicas
    blocks = key_grad.reshape(key_grad.shape[0], replicas, width)
    stacked_grads = jnp.einsum(
        "td,tbc->bdc", layer_inputs, blocks, preferred_element_type=jnp.float32
    )
    stacked_grads = stacked_grads.reshape(replicas * layer_inputs.shape[1], width)
    joint_grad = lax.psum_scatter(stacked_grads, ("rep", "fsdp"), scatter_dimension=0, tiled=True)
    local_sum = lax.psum_scatter(own_local, "rep", scatter_dimension=1, tiled=True)
    offset = lax.axis_index("rep") * width
    global_part = lax.dynamic_slice_in_dim(global_params, offset, width, 1)
    momentum_part = lax.dynamic_slice_in_dim(outer_momentum, offset, width, 1)
    outer_grad = global_part - (local_sum - inner_rate * joint_grad) / replicas
    momentum_next = outer_beta * momentum_part + outer_grad
    params_next = global_part - outer_rate * (outer_grad + outer_beta * momentum_next)
    fresh_params, fresh_momentum = (
        lax.all_gather(params_next.astype(jnp.bfloat16), "rep", axis=1, tiled=True).astype(
            params_next.dtype
        ),
        lax.all_gather(momentum_next.astype(jnp.bfloat16), "rep", axis=1, tiled=True).astype(
            momentum_next.dtype
        ),
    )
    weights_low = fresh_params.astype(jnp.bfloat16)
    projected = jnp.dot(
        next_inputs,
        lax.all_gather(weights_low, "fsdp", axis=0, tiled=True),
        preferred_element_type=jnp.float32,
    )
    return (fresh_params, fresh_momentum, projected.astype(jnp.bfloat16))


def solution(mesh):
    return jax.shard_map(
        body,
        mesh=mesh,
        in_specs=(
            P(("rep", "fsdp"), None),
            P(("rep", "fsdp"), None),
            P(("rep", "fsdp"), None),
            P(("rep", "fsdp"), None),
            P(("rep", "fsdp"), None),
            P("fsdp", None),
            P("rep", "fsdp", None),
            P("fsdp", None),
            P(("rep", "fsdp"), None),
        ),
        out_specs=(P("fsdp", None), P("fsdp", None), P(("rep", "fsdp"), None)),
        check_vma=False,
    )
```

profile of v0, /device:TPU:0, one launch (start us, length us, event | category | flops | bytes accessed | tf_op | source)
XLA Modules:
  0.0 467.8 jit_solution(7028264921164252495)
XLA Ops:
  7.2 0.0 copy-start
  7.2 0.0 reduce-scatter.3.cloned.1.call-start
  7.2 0.7 reduce-scatter.3.cloned.1.call-update
  7.9 0.0 reduce-scatter.5.cloned.1.call-start
  8.0 1.5 copy.35
  9.4 1.9 copy.36
  11.4 2.6 reshape.90
  14.0 0.0 copy-start.2
  14.0 1.2 copy.37
  15.2 3.7 fusion.19
  18.9 0.0 copy-done.2
  18.9 2.7 fusion.16
  21.6 4.8 %fusion.5 = f32[8,2,256,256]{2,3,1,0:T(8,128)} fusion(pred[256,256]{0,1:T(8,128)(4,1)S(1)} %iota_compare_fusion, bf16[256,8,2,128]{0,3,2,1:T(8,128)(2,1)S(1)} %bitcast.64, bf16[256,8,128,1]{2,1,0,3:T(8,128)(2,1)} %bitcast.69), kind=kOutput, calls=%fused_computation.11 | convolution fusion | flops 272634112 | bytes 5832704 | tf_op jit(solution)/shard_map/div | solution.py:48
  26.4 10.3 %fusion.14 = f32[256,8,128]{0,2,1:T(8,128)} fusion(bf16[256,8,2,128]{0,3,2,1:T(8,128)(2,1)S(1)} %bitcast.65, f32[8,2,256,256]{2,3,1,0:T(8,128)} %fusion.5, f32[8,256,256,2]{2,1,3,0:T(8,128)} %fusion.16, f32[8,256,256,2]{2,1,3,0:T(8,128)} %fusion.19), kind=kOutput, calls=%fused_computation.20 | convolution fusion | flops 277876992 | bytes 14680064 | tf_op jit(solution)/shard_map/hgij,ihgd->jhd/dot_general | solution.py:54
  36.7 0.3 multiply_cosine_fusion
  37.0 1.3 add_convert_fusion
  38.4 0.0 copy-done
  38.4 8.0 %convolution_bitcast_fusion = f32[4,4608,256]{1,2,0:T(8,128)} fusion(bf16[256,4,256]{0,2,1:T(8,128)(2,1)S(1)} %bitcast.67, bf16[256,4608]{1,0:T(8,128)(2,1)S(1)} %copy-done), kind=kOutput, calls=%fused_computation.2 | convolution fusion | flops 2415919104 | bytes 21757952 | tf_op jit(solution)/shard_map/td,tbc->bdc/dot_general | solution.py:75
  46.4 18.6 %copy.25 = f32[4,4608,256]{2,1,0:T(8,128)} copy(f32[4,4608,256]{1,2,0:T(8,128)} %convolution_bitcast_fusion) | data formatting | bytes 37748736 | tf_op jit(solution)/shard_map/td,tbc->bdc/transpose | solution.py:75
  65.1 0.0 reduce-scatter.5.cloned.1.call-update
  65.1 0.0 all-gather.4.cloned.1.call-start
  65.1 0.0 reduce-scatter.3.cloned.1.call-done
  65.2 209.6 %reduce-scatter.5.cloned.1.call-done = f32[576,256]{1,0:T(8,128)} async-done(((f32[18432,256]{1,0:T(8,128)}), f32[576,256]{1,0:T(8,128)}) %reduce-scatter.5.cloned.1.call-update) | async-done | bytes 589840 | tf_op jit(solution)/shard_map/reduce_scatter | solution.py:79
  274.7 2.6 fusion.21
  277.4 0.0 all-gather.4.cloned.1.call-update
  277.4 0.0 all-gather.6.cloned.1.call-start
  277.4 0.5 all-gather.6.cloned.1.call-update
  278.0 0.0 all-gather.8.cloned.1.call-start
  278.0 16.2 %all-gather.4.cloned.1.call-done = bf16[576,1024]{1,0:T(8,128)(2,1)} async-done(((bf16[576,256]{1,0:T(8,128)(2,1)}), bf16[576,1024]{1,0:T(8,128)(2,1)}) %all-gather.4.cloned.1.call-update) | async-done | bytes 1179664 | tf_op jit(solution)/shard_map/all_gather | solution.py:88
  294.2 0.0 all-gather.8.cloned.1.call-update
  294.3 3.0 convert_element_type.58
  297.2 16.6 %all-gather.6.cloned.1.call-done = bf16[576,1024]{1,0:T(8,128)(2,1)} async-done(((bf16[576,256]{1,0:T(8,128)(2,1)}), bf16[576,1024]{1,0:T(8,128)(2,1)}) %all-gather.6.cloned.1.call-update) | async-done | bytes 1179664 | tf_op jit(solution)/shard_map/all_gather | solution.py:91
  313.8 3.0 convert_element_type.60
  316.8 136.4 %all-gather.8.cloned.1.call-done = bf16[4608,1024]{1,0:T(8,128)(2,1)} async-done(((bf16[576,1024]{1,0:T(8,128)(2,1)}), bf16[4608,1024]{1,0:T(8,128)(2,1)}) %all-gather.8.cloned.1.call-update) | async-done | bytes 9437200 | tf_op jit(solution)/shard_map/all_gather | solution.py:98
  453.1 0.0 copy-start.1
  453.1 7.1 %fusion.15 = bf16[256,1024]{0,1:T(8,128)(2,1)S(1)} fusion(bf16[4608,1024]{1,0:T(8,128)(2,1)} %all-gather.8.cloned.1.call-done, bf16[256,4608]{1,0:T(8,128)(2,1)} %param.17), kind=kOutput, calls=%fused_computation.22 | convolution fusion | flops 2416181248 | bytes 12320768 | tf_op jit(solution)/shard_map/dot_general | solution.py:96
  460.3 1.0 copy.26
  461.3 0.0 copy-done.1
  (4 shorter events, 0.1 us)
Async XLA Ops:
  7.2 31.2 %copy-start = (bf16[256,4608]{1,0:T(8,128)(2,1)S(1)}, bf16[256,4608]{1,0:T(8,128)(2,1)}, u32[]{:S(2)}) copy-start(bf16[256,4608]{1,0:T(8,128)(2,1)} %param.9) | copy-start | bytes 7077892
  7.2 58.0 %reduce-scatter.3.cloned.1.call-start = ((), (), s32[]{:S(2)}) async-start(), calls=%async_computation.2 | async-start | bytes 2949120 | tf_op jit(solution)/shard_map/reduce_scatter | solution.py:80
  7.9 266.8 %reduce-scatter.5.cloned.1.call-start = ((), (), s32[]{:S(2)}) async-start(), calls=%async_computation.3 | async-start | bytes 19464192 | tf_op jit(solution)/shard_map/reduce_scatter | solution.py:79
  14.0 5.0 %copy-start.2 = (bf16[256,8,2,128]{3,2,1,0:T(2,128)(2,1)S(1)}, bf16[256,8,2,128]{3,2,1,0:T(2,128)(2,1)}, u32[]{:S(2)}) copy-start(bf16[256,8,2,128]{3,2,1,0:T(2,128)(2,1)} %reshape.90) | copy-start | bytes 3145732
  65.1 229.2 %all-gather.4.cloned.1.call-start = ((), (), s32[]{:S(2)}) async-start(), calls=%async_computation.4 | async-start | bytes 1474560 | tf_op jit(solution)/shard_map/all_gather | solution.py:88
  277.4 36.4 %all-gather.6.cloned.1.call-start = ((), (), s32[]{:S(2)}) async-start(), calls=%async_computation.5 | async-start | bytes 1474560 | tf_op jit(solution)/shard_map/all_gather | solution.py:91
  278.0 175.2 %all-gather.8.cloned.1.call-start = ((), (), s32[]{:S(2)}) async-start(), calls=%async_computation.6 | async-start | bytes 10616832 | tf_op jit(solution)/shard_map/all_gather | solution.py:98
  453.1 8.2 %copy-start.1 = (bf16[256,4608]{1,0:T(8,128)(2,1)S(1)}, bf16[256,4608]{1,0:T(8,128)(2,1)}, u32[]{:S(2)}) copy-start(bf16[256,4608]{1,0:T(8,128)(2,1)} %param.9) | copy-start | bytes 7077892
Sparse Core Ops, SparseCore 0:
  10.5 35.4 reduce-scatter.2
  65.2 209.4 reduce-scatter.4
  277.5 16.6 all-gather.3
  296.2 17.5 all-gather.5
  315.9 137.2 all-gather.7
where the time goes:
time: 468 us
  waiting for transfers between devices  380 us (81%)
  matrix products  36.6 us (8%)
  local copies, waits for them, and re-layouts  26.9 us (6%)
  between operations  13.9 us (3%)
  other arithmetic  10.3 us (2%)
    reduce_scatter x1, waiting for transfers between devices, body(): lax.psum_scatter(stacked_grads, ('rep', 'fsdp'), scatter_dimension=0, til...  210 us
    all_gather x1, waiting for transfers between devices, body(): lax.all_gather(weights_low, 'fsdp', axis=0, tiled=True)  136 us
    transpose x1, local copies, waits for them, and re-layouts, body(): jnp.einsum('td,tbc->bdc', layer_inputs, blocks, preferred_element_type=jn...  18.6 us
    all_gather x1, waiting for transfers between devices, body(): lax.all_gather(momentum_next.astype(jnp.bfloat16), 'rep', axis=1, tiled=T...  16.6 us
    all_gather x1, waiting for transfers between devices, body(): lax.all_gather(params_next.astype(jnp.bfloat16), 'rep', axis=1, tiled=True)  16.2 us
    dot_general x1, matrix products, attention_keys(): jnp.einsum('hgij,ihgd->jhd', dlogits, query_wide, preferred_element_type=...  10.3 us
  transfers between devices with their start and end apart: 5, of which 4 were waited for; matrix products, arithmetic and copies ran while one was open for 13% of the time, Pallas kernels for 0%

commit v1 on v0

--- a/solution.py
+++ b/solution.py
@@ -1,6 +1,10 @@
+import functools
+
 import jax
 import jax.numpy as jnp
 from jax import lax
+from jax.experimental import pallas as pl
+from jax.experimental.pallas import tpu as pltpu
 from jax.sharding import PartitionSpec as P
 
 QH = 16
@@ -14,6 +18,8 @@
 inner_rate = 0.02
 outer_rate = 0.7
 outer_beta = 0.9
+
+MESH = pl.DeviceIdType.MESH
 
 
 def rotate_back(grads, length):
@@ -54,6 +60,201 @@
     rotated = jnp.einsum("hgij,ihgd->jhd", dlogits, query_wide, preferred_element_type=jnp.float32)
     plain = rotate_back(rotated, length)
     return plain.reshape(length, KVH * HD).astype(jnp.bfloat16)
+
+
+def outer_kernel(
+    part, glob, mom, weights, fresh, rc, r1a, r1b, r2a, r2b, s3, r3, send_sem, recv_sem
+):
+    lines, _, rows, cols = part.shape
+    half, quarter, eighth = cols // 2, cols // 4, cols // 8
+    rep, fsdp = lax.axis_index("rep"), lax.axis_index("fsdp")
+    core, x = lax.rem(rep, 2), rep // 2
+    y, z = lax.rem(fsdp, 2), fsdp // 2
+    over_core = {"rep": rep + 1 - 2 * core}
+    over_x = {"rep": rep + 2 - 4 * x}
+    over_y = {"fsdp": fsdp + 1 - 2 * y}
+
+    def over_z(line):
+        return {"fsdp": line * 2 + y}
+
+    def at(start, size):
+        return pl.ds(pl.multiple_of(start, size), size)
+
+    f32 = jnp.float32
+    peers = [over_core, over_x, over_y] + [
+        over_z(lax.rem(z + t, lines)) for t in range(1, lines)
+    ]
+    barrier = pltpu.get_barrier_semaphore()
+    for peer in peers:
+        pl.semaphore_signal(barrier, inc=1, device_id=peer, device_id_type=MESH)
+    pl.semaphore_wait(barrier, len(peers))
+
+    copies = {}
+
+    def send(kind, step, src, dst, peer):
+        slot = len(copies)
+        copy = pltpu.make_async_remote_copy(
+            src_ref=src,
+            dst_ref=dst,
+            send_sem=send_sem.at[slot],
+            recv_sem=recv_sem.at[slot],
+            device_id=peer,
+            device_id_type=MESH,
+        )
+        copy.start()
+        copies[kind, step] = copy
+
+    def arrive(kind, step):
+        copies[kind, step].wait_recv()
+
+    def line_of(step):
+        return lax.rem(z + 1 + step, lines)
+
+    for s in range(lines):
+        g = line_of(s)
+        send("c", s, part.at[g, :, :, at((1 - core) * half, half)], rc.at[g], over_core)
+
+    def sum_core(s):
+        g = line_of(s)
+        arrive("c", s)
+        for yy in range(2):
+            mine = part[g, yy, :, at(core * half, half)]
+            rc[g, yy] = (rc[g, yy].astype(f32) + mine.astype(f32)).astype(rc.dtype)
+        send("1a", s, rc.at[g, :, :, at((1 - x) * eighth, eighth)], r1a.at[g], over_x)
+        send("1b", s, rc.at[g, 1 - y, :, quarter:half], r1b.at[g], over_y)
+
+    def sum_first(s):
+        g = line_of(s)
+        arrive("1a", s)
+        for yy in range(2):
+            mine = rc[g, yy, :, at(x * eighth, eighth)]
+            r1a[g, yy] = (r1a[g, yy].astype(f32) + mine.astype(f32)).astype(rc.dtype)
+        send("2a", s, r1a.at[g, 1 - y], r2a.at[g], over_y)
+        arrive("1b", s)
+        mine = rc[g, y, :, quarter:half]
+        r1b[g] = (r1b[g].astype(f32) + mine.astype(f32)).astype(rc.dtype)
+        send("2b", s, r1b.at[g, :, at((1 - x) * eighth, eighth)], r2b.at[g], over_x)
+
+    def sum_second(s):
+        g = line_of(s)
+        arrive("2a", s)
+        sum_a = r2a[g].astype(f32) + r1a[g, y].astype(f32)
+        arrive("2b", s)
+        sum_b = r2b[g].astype(f32) + r1b[g, :, at(x * eighth, eighth)].astype(f32)
+        if s == lines - 1:
+            return sum_a, sum_b
+        s3[s, :, :eighth] = sum_a.astype(s3.dtype)
+        s3[s, :, eighth:] = sum_b.astype(s3.dtype)
+        send("3", s, s3.at[s], r3.at[s], over_z(g))
+
+    for tick in range(lines + 2):
+        if 0 <= tick - 2:
+            own = sum_second(tick - 2)
+        if 0 <= tick - 1 < lines:
+            sum_first(tick - 1)
+        if tick < lines:
+            sum_core(tick)
+
+    col_a = at(core * half + x * eighth, eighth)
+    col_b = at(core * half + quarter + x * eighth, eighth)
+    for s in range(lines - 1):
+        arrive("3", s)
+    for n, col in enumerate((col_a, col_b)):
+        total = own[n]
+        for s in range(lines - 1):
+            total = total + r3[s, :, n * eighth : (n + 1) * eighth].astype(f32)
+        outer_grad = total * 0.25
+        momentum = outer_beta * mom[:, col] + outer_grad
+        fresh[:, col] = momentum.astype(fresh.dtype)
+        params = glob[:, col] - outer_rate * (outer_grad + outer_beta * momentum)
+        weights[z, y, :, col] = params.astype(weights.dtype)
+
+    def swap(kind, step, ref, peer):
+        send(kind, step, ref, ref, peer)
+
+    def from_line(step):
+        return lax.rem(z + lines - step, lines)
+
+    for t in range(1, lines):
+        peer = over_z(lax.rem(z + t, lines))
+        swap("g3a", t, weights.at[z, y, :, col_a], peer)
+        swap("g3b", t, weights.at[z, y, :, col_b], peer)
+
+    def landed(kind, step, ref):
+        copy = copies[kind, step]
+        copy.wait_recv()
+
+    def gather_third(t):
+        g = from_line(t)
+        if t:
+            landed("g3a", t, None)
+        swap("g2a", t, weights.at[g, y, :, col_a], over_y)
+        if t:
+            landed("g3b", t, None)
+        swap("g2b", t, weights.at[g, y, :, col_b], over_x)
+        if not t:
+            swap("ma", 0, fresh.at[:, col_a], over_x)
+            swap("mb", 0, fresh.at[:, col_b], over_x)
+
+    def gather_second(t):
+        g = from_line(t)
+        arrive("g2a", t)
+        swap("g1a", t, weights.at[g, :, :, col_a], over_x)
+        arrive("g2b", t)
+        swap("g1b", t, weights.at[g, y, :, at(core * half + quarter, quarter)], over_y)
+
+    def gather_first(t):
+        g = from_line(t)
+        arrive("g1a", t)
+        arrive("g1b", t)
+        swap("gc", t, weights.at[g, :, :, at(core * half, half)], over_core)
+
+    for tick in range(lines + 2):
+        if 0 <= tick - 2:
+            gather_first(tick - 2)
+        if 0 <= tick - 1 < lines:
+            gather_second(tick - 1)
+        if tick < lines:
+            gather_third(tick)
+    arrive("ma", 0)
+    arrive("mb", 0)
+    swap("mc", 0, fresh.at[:, at(core * half, half)], over_core)
+    for t in range(lines):
+        arrive("gc", t)
+    arrive("mc", 0)
+    for copy in copies.values():
+        copy.wait_send()
+
+
+def outer_step(part, glob, mom):
+    lines, pair, rows, cols = part.shape
+    low = jnp.bfloat16
+    half, quarter, eighth = cols // 2, cols // 4, cols // 8
+    count = lines * 5 + lines - 1 + 2 * (lines - 1) + lines * 5 + 3
+    vmem = pl.BlockSpec(memory_space=pltpu.VMEM)
+    return pl.pallas_call(
+        outer_kernel,
+        out_shape=(
+            jax.ShapeDtypeStruct(part.shape, low),
+            jax.ShapeDtypeStruct((rows, cols), low),
+        ),
+        in_specs=[vmem] * 3,
+        out_specs=(vmem, vmem),
+        scratch_shapes=[
+            pltpu.VMEM((lines, pair, rows, half), low),
+            pltpu.VMEM((lines, pair, rows, eighth), low),
+            pltpu.VMEM((lines, rows, quarter), low),
+            pltpu.VMEM((lines, rows, eighth), low),
+            pltpu.VMEM((lines, rows, eighth), low),
+            pltpu.VMEM((lines - 1, rows, quarter), low),
+            pltpu.VMEM((lines - 1, rows, quarter), low),
+            pltpu.SemaphoreType.DMA((count,)),
+            pltpu.SemaphoreType.DMA((count,)),
+        ],
+        compiler_params=pltpu.CompilerParams(
+            collective_id=0, has_side_effects=True, vmem_limit_bytes=60 * 2**20
+        ),
+    )(part, glob, mom)
 
 
 def body(
@@ -68,37 +269,28 @@
     next_inputs,
 ):
     key_grad = attention_keys(queries, saved_keys, saved_values, out_grad)
-    replicas = lax.axis_size("rep")
-    own_local = replica_params[0]
-    width = key_grad.shape[1] // replicas
-    blocks = key_grad.reshape(key_grad.shape[0], replicas, width)
-    stacked_grads = jnp.einsum(
-        "td,tbc->bdc", layer_inputs, blocks, preferred_element_type=jnp.float32
-    )
-    stacked_grads = stacked_grads.reshape(replicas * layer_inputs.shape[1], width)
-    joint_grad = lax.psum_scatter(stacked_grads, ("rep", "fsdp"), scatter_dimension=0, tiled=True)
-    local_sum = lax.psum_scatter(own_local, "rep", scatter_dimension=1, tiled=True)
-    offset = lax.axis_index("rep") * width
-    global_part = lax.dynamic_slice_in_dim(global_params, offset, width, 1)
-    momentum_part = lax.dynamic_slice_in_dim(outer_momentum, offset, width, 1)
-    outer_grad = global_part - (local_sum - inner_rate * joint_grad) / replicas
-    momentum_next = outer_beta * momentum_part + outer_grad
-    params_next = global_part - outer_rate * (outer_grad + outer_beta * momentum_next)
-    fresh_params, fresh_momentum = (
-        lax.all_gather(params_next.astype(jnp.bfloat16), "rep", axis=1, tiled=True).astype(
-            params_next.dtype
-        ),
-        lax.all_gather(momentum_next.astype(jnp.bfloat16), "rep", axis=1, tiled=True).astype(
-            momentum_next.dtype
-        ),
-    )
-    weights_low = fresh_params.astype(jnp.bfloat16)
-    projected = jnp.dot(
-        next_inputs,
-        lax.all_gather(weights_low, "fsdp", axis=0, tiled=True),
-        preferred_element_type=jnp.float32,
-    )
-    return (fresh_params, fresh_momentum, projected.astype(jnp.bfloat16))
+    shards = lax.axis_size("fsdp")
+    mine = lax.axis_index("fsdp")
+    rows, cols = global_params.shape
+    drift = global_params - replica_params[0]
+    partial = inner_rate * lax.dot_general(
+        layer_inputs, key_grad, (((0,), (0,)), ((), ())), preferred_element_type=jnp.float32
+    )
+    partial = partial.astype(jnp.bfloat16)
+    block = lax.dynamic_slice_in_dim(partial, mine * rows, rows, 0)
+    block = (block.astype(jnp.float32) + drift).astype(jnp.bfloat16)
+    partial = lax.dynamic_update_slice_in_dim(partial, block, mine * rows, 0)
+    weights, momentum = outer_step(
+        partial.reshape(shards // 2, 2, rows, cols), global_params, outer_momentum
+    )
+    weights = weights.reshape(shards * rows, cols)
+    projected = jnp.dot(next_inputs, weights, preferred_element_type=jnp.float32)
+    own = lax.dynamic_slice_in_dim(weights, mine * rows, rows, 0)
+    return (
+        own.astype(jnp.float32),
+        momentum.astype(jnp.float32),
+        projected.astype(jnp.bfloat16),
+    )
 
 
 def solution(mesh):

time: 468 us -> 204 us (0.44)
  waiting for transfers between devices: 380 us -> 0 us
  Pallas kernels: 0 us -> 116 us
  local copies, waits for them, and re-layouts: 26.9 us -> 44.9 us
  between operations: 13.9 us -> 0.75 us
    reduce_scatter x2 -> x0, waiting for transfers between devices: 210 us -> none  [the longest x1 210 us: body(): lax.psum_scatter(stacked_grads, ('rep', 'fsdp'), scatter_dimension=0, til...]
    all_gather x3 -> x0, waiting for transfers between devices: 169 us -> none  [the longest x1 136 us: body(): lax.all_gather(weights_low, 'fsdp', axis=0, tiled=True)]
    pallas_call x0 -> x1, Pallas kernels: none -> 116 us  [outer_step(): pl.pallas_call(outer_kernel, out_shape=(jax.ShapeDtypeStruct(part.shape,...]
    dynamic_update_slice x0 -> x2, local copies, waits for them, and re-layouts: none -> 25 us  [body(): partial = lax.dynamic_update_slice_in_dim(partial, block, mine * rows, 0)]
    transpose x1 -> x0, local copies, waits for them, and re-layouts: 18.6 us -> none  [body(): jnp.einsum('td,tbc->bdc', layer_inputs, blocks, preferred_element_type=jn...]
    unnamed x9 -> x17, local copies, waits for them, and re-layouts: 4.18 us -> 15.9 us
  transfers between devices with their start and end apart: 5 -> 0, of which waited for: 4 -> 0; matrix products, arithmetic and copies ran while one was open for 13% -> 0% of each run, Pallas kernels for 0% -> 0%
where the time goes in v1:
time: 204 us; the launch traced here: 203 us
  Pallas kernels  116 us (57%)
  local copies, waits for them, and re-layouts  44.9 us (22%)
  matrix products  33.1 us (16%)
  other arithmetic  7.9 us (4%)
    pallas_call x1, Pallas kernels, outer_step(): pl.pallas_call(outer_kernel, out_shape=(jax.ShapeDtypeStruct(part.shape,...  116 us
    dynamic_update_slice x2, local copies, waits for them, and re-layouts, body(): partial = lax.dynamic_update_slice_in_dim(partial, block, mine * rows, 0)  25 us
    unnamed x17, local copies, waits for them, and re-layouts  15.9 us
    dot_general x1, matrix products, attention_keys(): jnp.einsum('hgij,ihgd->jhd', dlogits, query_wide, preferred_element_type=...  9.86 us
    dot_general x1, matrix products, body(): jnp.dot(next_inputs, weights, preferred_element_type=jnp.float32)  7.94 us
    div x1, matrix products, attention_keys(): probs = unnormed / jnp.sum(unnormed, axis=-1, keepdims=True)  4.79 us

profile of v1, /device:TPU:0, one launch (start us, length us, event | category | flops | bytes accessed | tf_op | source)
XLA Modules:
  0.0 202.5 jit_solution(11626339751798531888)
XLA Ops:
  0.6 0.0 copy-start
  0.7 0.6 iota_compare_fusion
  1.3 0.3 multiply_cosine_fusion
  1.6 1.9 copy.31
  3.6 1.9 copy.32
  5.5 1.5 copy.30
  7.0 2.6 %reshape.91 = bf16[256,8,2,128]{3,2,1,0:T(2,128)(2,1)} reshape(bf16[256,2048]{1,0:T(8,128)(2,1)} %param.13) | data formatting | bytes 2097152 | tf_op jit(solution)/shard_map/reshape | solution.py:45
  9.6 4.1 %fusion.17 = f32[8,256,256,2]{2,1,3,0:T(8,128)} fusion(bf16[256,8,2,128]{3,2,1,0:T(2,128)(2,1)} %reshape.91, bf16[256,8,128,1]{2,1,0,3:T(8,128)(2,1)} %bitcast.74), kind=kOutput, calls=%fused_computation.26 | convolution fusion | flops 268435456 | bytes 5767168 | tf_op jit(solution)/shard_map/ihgd,jhd->hgij/dot_general | solution.py:55
  13.6 3.1 %copy.18 = f32[1,576,1024]{1,2,0:T(8,128)} copy(f32[1,576,1024]{2,1,0:T(8,128)} %param.15) | data formatting | bytes 4718592 | tf_op args[6]
  16.8 3.2 %copy.19 = f32[576,1024]{0,1:T(8,128)} copy(f32[576,1024]{1,0:T(8,128)} %glob.1) | data formatting | bytes 4718592 | tf_op args[5]
  19.9 4.8 %fusion.7 = f32[8,2,256,256]{2,3,1,0:T(8,128)} fusion(pred[256,256]{0,1:T(8,128)(4,1)} %iota_compare_fusion, bf16[256,8,2,128]{0,3,2,1:T(8,128)(2,1)S(1)} %bitcast.69, bf16[256,8,128,1]{2,1,0,3:T(8,128)(2,1)} %bitcast.72), kind=kOutput, calls=%fused_computation.14 | convolution fusion | flops 272634112 | bytes 5832704 | tf_op jit(solution)/shard_map/div | solution.py:54
  24.7 3.7 %fusion.20 = f32[8,256,256,2]{2,1,3,0:T(8,128)} fusion(bf16[256,8,2,128]{0,3,2,1:T(8,128)(2,1)S(1)} %bitcast.70, bf16[256,8,128,1]{2,1,0,3:T(8,128)(2,1)} %bitcast.73), kind=kOutput, calls=%fused_computation.30 | convolution fusion | flops 268435456 | bytes 5767168 | tf_op jit(solution)/shard_map/ihgd,jhd->hgij/dot_general | solution.py:47
  28.4 9.9 %fusion.15 = f32[256,8,128]{0,2,1:T(8,128)} fusion(bf16[256,8,2,128]{0,3,2,1:T(8,128)(2,1)S(1)} %bitcast.71, f32[8,2,256,256]{2,3,1,0:T(8,128)} %fusion.7, f32[8,256,256,2]{2,1,3,0:T(8,128)} %fusion.17, f32[8,256,256,2]{2,1,3,0:T(8,128)} %fusion.20), kind=kOutput, calls=%fused_computation.22 | convolution fusion | flops 277876992 | bytes 14680064 | tf_op jit(solution)/shard_map/hgij,ihgd->jhd/dot_general | solution.py:60
  38.2 1.3 add_convert_fusion
  39.6 0.0 copy-done
  39.6 0.0 copy-start.3
  39.6 0.0 copy-start.4
  39.7 2.8 %multiply_convert_fusion = bf16[1024,4608]{1,0:T(8,128)(2,1)S(1)} fusion(bf16[256,1024]{0,1:T(8,128)(2,1)S(1)} %bitcast.77, bf16[256,4608]{1,0:T(8,128)(2,1)S(1)} %copy-done), kind=kOutput, calls=%fused_computation.2 | convolution fusion | flops 2425356288 | bytes 12320768 | tf_op jit(solution)/shard_map/dot_general | solution.py:276
  42.5 0.0 copy-start.2
  42.5 3.6 %copy-done.2 = bf16[1024,4608]{1,0:T(8,128)(2,1)} copy-done((bf16[1024,4608]{1,0:T(8,128)(2,1)}, bf16[1024,4608]{1,0:T(8,128)(2,1)S(1)}, u32[]{:S(2)}) %copy-start.2) | copy-done | bytes 9437208
  46.1 0.0 copy-done.3
  46.1 0.0 copy-done.4
  46.1 0.8 fusion.6
  46.9 12.4 %dynamic_update_slice.3 = bf16[4608,1024]{0,1:T(8,128)(2,1)} dynamic-update-slice(bf16[4608,1024]{0,1:T(8,128)(2,1)} %bitcast.68, bf16[576,1024]{0,1:T(8,128)(2,1)S(1)} %fusion.6, s32[]{:T(128)S(6)} %select_n.10, s32[]{:T(128)} %constant.24.clone.1) | dynamic-update-slice | bytes 2359300 | tf_op jit(solution)/shard_map/dynamic_update_slice | solution.py:282
  59.3 12.7 %copy.20 = bf16[4608,1024]{1,0:T(8,128)(2,1)} copy(bf16[4608,1024]{0,1:T(8,128)(2,1)} %dynamic_update_slice.3) | data formatting | bytes 18874368 | tf_op jit(solution)/shard_map/dynamic_update_slice | solution.py:282
  72.0 115.8 %shard_map.112 = (bf16[4,2,576,1024]{3,2,1,0:T(8,128)(2,1)}, bf16[576,1024]{1,0:T(8,128)(2,1)}) custom-call(bf16[4,2,576,1024]{3,2,1,0:T(8,128)(2,1)} %bitcast.67, f32[576,1024]{1,0:T(8,128)} %glob.1, f32[576,1024]{1,0:T(8,128)} %mom.1), custom_call_target="tpu_custom_call" | custom-call | tf_op jit(solution)/shard_map/pallas_call | solution.py:235
  187.8 0.0 copy-start.1
  187.8 7.9 %fusion.16 = bf16[256,1024]{0,1:T(8,128)(2,1)} fusion(bf16[4608,1024]{1,0:T(8,128)(2,1)} %bitcast.78, bf16[256,4608]{1,0:T(8,128)(2,1)} %param.17), kind=kOutput, calls=%fused_computation.24 | convolution fusion | flops 2416181248 | bytes 12320768 | tf_op jit(solution)/shard_map/dot_general | solution.py:287
  195.7 0.0 copy-start.5
  195.7 3.1 %dynamic-slice_convert_fusion = f32[576,1024]{1,0:T(8,128)} fusion(bf16[4608,1024]{1,0:T(8,128)(2,1)} %bitcast.79, s32[]{:T(128)S(6)} %select_n.10), kind=kLoop, calls=%fused_computation.25 | loop fusion | flops 589824 | bytes 3538948 | tf_op jit(solution)/shard_map/convert_element_type | solution.py:290
  198.8 2.0 %copy.21 = bf16[256,1024]{1,0:T(8,128)(2,1)} copy(bf16[256,1024]{0,1:T(8,128)(2,1)} %fusion.16) | data formatting | bytes 1048576
  200.8 0.0 copy-done.5
  200.8 1.7 convert_element_type.70
  202.5 0.0 copy-done.1
  (3 shorter events, 0.0 us)
Async XLA Ops:
  0.6 39.0 %copy-start = (bf16[256,4608]{1,0:T(8,128)(2,1)S(1)}, bf16[256,4608]{1,0:T(8,128)(2,1)}, u32[]{:S(2)}) copy-start(bf16[256,4608]{1,0:T(8,128)(2,1)} %param.9) | copy-start | bytes 7077892
  39.6 6.5 %copy-start.3 = (f32[1,576,1024]{1,2,0:T(8,128)S(1)}, f32[1,576,1024]{1,2,0:T(8,128)}, u32[]{:S(2)}) copy-start(f32[1,576,1024]{1,2,0:T(8,128)} %copy.18) | copy-start | bytes 7077892
  39.6 6.5 %copy-start.4 = (f32[576,1024]{0,1:T(8,128)S(1)}, f32[576,1024]{0,1:T(8,128)}, u32[]{:S(2)}) copy-start(f32[576,1024]{0,1:T(8,128)} %copy.19) | copy-start | bytes 7077892
  42.5 3.6 %copy-start.2 = (bf16[1024,4608]{1,0:T(8,128)(2,1)}, bf16[1024,4608]{1,0:T(8,128)(2,1)S(1)}, u32[]{:S(2)}) copy-start(bf16[1024,4608]{1,0:T(8,128)(2,1)S(1)} %multiply_convert_fusion) | copy-start | bytes 28311556
  187.8 14.7 %copy-start.1 = (bf16[256,4608]{1,0:T(8,128)(2,1)S(1)}, bf16[256,4608]{1,0:T(8,128)(2,1)}, u32[]{:S(2)}) copy-start(bf16[256,4608]{1,0:T(8,128)(2,1)} %param.9) | copy-start | bytes 7077892
  195.7 5.1 %copy-start.5 = (bf16[576,1024]{1,0:T(8,128)(2,1)S(1)}, bf16[576,1024]{1,0:T(8,128)(2,1)}, u32[]{:S(2)}) copy-start(bf16[576,1024]{1,0:T(8,128)(2,1)} %get-tuple-element.6) | copy-start | bytes 3538948

commit v2 on v1

v2 whole, which is shorter than its diff:
```python
import functools

import jax
import jax.numpy as jnp
import numpy as np
from jax import lax
from jax.experimental import pallas as pl
from jax.experimental.pallas import tpu as pltpu
from jax.sharding import PartitionSpec as P

QH = 16
KVH = 8
HD = 128


score_scale = 1.0 / 12.0
soft_cap = 50.0
rope_base = 10000.0
inner_rate = 0.02
outer_rate = 0.7
outer_beta = 0.9

MESH = pl.DeviceIdType.MESH


def attention_kernel(q_ref, k_ref, v_ref, g_ref, cos_ref, sin_ref, out_ref):
    length = k_ref.shape[0]
    f32 = jnp.float32
    keys, values = k_ref[...], v_ref[...]
    row = lax.broadcasted_iota(jnp.int32, (length, length), 0)
    column = lax.broadcasted_iota(jnp.int32, (length, length), 1)
    causal = row >= column
    across = (((1,), (1,)), ((), ()))
    rotated = jnp.zeros((length, HD), f32)
    for j in range(QH // KVH):
        cols = slice(j * HD, (j + 1) * HD)
        query = q_ref[:, cols]
        logits = lax.dot_general(query, keys, across, preferred_element_type=f32)
        capped = jnp.tanh(logits * (score_scale / soft_cap))
        unnormed = jnp.where(causal, jnp.exp(soft_cap * capped), 0.0)
        probs = unnormed / jnp.sum(unnormed, axis=-1, keepdims=True)
        dprobs = lax.dot_general(g_ref[:, cols], values, across, preferred_element_type=f32)
        center = jnp.sum(probs * dprobs, axis=-1, keepdims=True)
        dlogits = probs * (dprobs - center) * (1.0 - capped * capped) * score_scale
        rotated += lax.dot_general(
            dlogits.astype(jnp.bfloat16),
            query,
            (((0,), (0,)), ((), ())),
            preferred_element_type=f32,
        )
    swapped = jnp.concatenate([rotated[:, HD // 2 :], rotated[:, : HD // 2]], axis=-1)
    out_ref[...] = (rotated * cos_ref[...] + swapped * sin_ref[...]).astype(out_ref.dtype)


def attention_keys(query_rows, key_rows, value_rows, grad_rows):
    length = query_rows.shape[0]
    group = QH // KVH
    half = HD // 2
    freqs = np.float32(rope_base) ** (-np.arange(half, dtype=np.float32) / np.float32(half))
    angles = (np.arange(length, dtype=np.float32)[:, None] * freqs[None, :]).astype(np.float64)
    cosine = np.concatenate([np.cos(angles)] * 2, axis=1).astype(np.float32)
    sine = np.concatenate([np.sin(angles), -np.sin(angles)], axis=1).astype(np.float32)
    wide = pl.BlockSpec((length, group * HD), lambda h: (0, h))
    narrow = pl.BlockSpec((length, HD), lambda h: (0, h))
    table = pl.BlockSpec((length, HD), lambda h: (0, 0))
    return pl.pallas_call(
        attention_kernel,
        grid=(KVH,),
        out_shape=jax.ShapeDtypeStruct((length, KVH * HD), jnp.bfloat16),
        in_specs=[wide, narrow, narrow, wide, table, table],
        out_specs=narrow,
    )(query_rows, key_rows, value_rows, grad_rows, jnp.asarray(cosine), jnp.asarray(sine))


def outer_kernel(inside, *refs):
    if inside:
        (layer, keyg, drift, nxt_in, glob_in, mom_in, fresh, own_out, proj) = refs[:9]
        (part, weights, nxt, total_ref, load_sem, *rest) = refs[9:]
    else:
        (part, glob_in, mom_in, fresh, weights, load_sem, *rest) = refs
    glob, mom, rc, r1a, r1b, r2a, r2b, s3, r3, send_sem, recv_sem = rest
    lines = part.shape[0]
    rows, cols = glob.shape
    half, quarter, eighth = cols // 2, cols // 4, cols // 8
    rep, fsdp = lax.axis_index("rep"), lax.axis_index("fsdp")
    core, x = lax.rem(rep, 2), rep // 2
    y, z = lax.rem(fsdp, 2), fsdp // 2
    over_core = {"rep": rep + 1 - 2 * core}
    over_x = {"rep": rep + 2 - 4 * x}
    over_y = {"fsdp": fsdp + 1 - 2 * y}
    every = slice(None)

    def over_z(line):
        return {"fsdp": line * 2 + y}

    def at(start, size):
        return pl.ds(pl.multiple_of(start, size), size)

    def pair(ref, g, col=every):
        return ref.at[g, :, col] if inside else ref.at[g, :, :, col]

    def block(ref, g, yy, col=every):
        if inside:
            return ref.at[g, at(yy * rows, rows), col]
        return ref.at[g, yy, :, col]

    loads = [
        pltpu.make_async_copy(src, dst, load_sem.at[n])
        for n, (src, dst) in enumerate(
            [(glob_in, glob), (mom_in, mom)] + ([(nxt_in, nxt)] if inside else [])
        )
    ]
    for load in loads:
        load.start()

    f32 = jnp.float32
    peers = [over_core, over_x, over_y] + [
        over_z(lax.rem(z + t, lines)) for t in range(1, lines)
    ]
    barrier = pltpu.get_barrier_semaphore()
    for peer in peers:
        pl.semaphore_signal(barrier, inc=1, device_id=peer, device_id_type=MESH)
    pl.semaphore_wait(barrier, len(peers))

    copies = {}

    def send(kind, step, src, dst, peer):
        slot = len(copies)
        copy = pltpu.make_async_remote_copy(
            src_ref=src,
            dst_ref=dst,
            send_sem=send_sem.at[slot],
            recv_sem=recv_sem.at[slot],
            device_id=peer,
            device_id_type=MESH,
        )
        copy.start()
        copies[kind, step] = copy

    def arrive(kind, step):
        copies[kind, step].wait_recv()

    def line_of(step):
        return lax.rem(z + 1 + step, lines)

    def multiply(s):
        g = line_of(s)
        if inside:
            width = 2 * rows
            tile = 128

            def one(n, carry):
                left = layer[:, at(g * width + n * tile, tile)]
                result = lax.dot_general(
                    left, keyg[...], (((0,), (0,)), ((), ())), preferred_element_type=f32
                )
                part[g, at(n * tile, tile), :] = (result * inner_rate).astype(part.dtype)
                return carry

            lax.fori_loop(0, width // tile, one, 0)
            if s == lines - 1:
                mine = block(part, g, y)
                mine[...] = (mine[...].astype(f32) + (glob[...] - drift[...])).astype(part.dtype)
        theirs = at((1 - core) * half, half)
        send("c", s, pair(part, g, theirs), pair(rc, g), over_core)

    def sum_core(s):
        g = line_of(s)
        arrive("c", s)
        for yy in range(2):
            mine = block(part, g, yy, at(core * half, half))[...]
            sums = block(rc, g, yy)
            sums[...] = (sums[...].astype(f32) + mine.astype(f32)).astype(rc.dtype)
        send("1a", s, pair(rc, g, at((1 - x) * eighth, eighth)), pair(r1a, g), over_x)
        send("1b", s, block(rc, g, 1 - y, slice(quarter, half)), r1b.at[g], over_y)

    def sum_first(s):
        g = line_of(s)
        arrive("1a", s)
        for yy in range(2):
            mine = block(rc, g, yy, at(x * eighth, eighth))[...]
            sums = block(r1a, g, yy)
            sums[...] = (sums[...].astype(f32) + mine.astype(f32)).astype(rc.dtype)
        send("2a", s, block(r1a, g, 1 - y), r2a.at[g], over_y)
        arrive("1b", s)
        mine = block(rc, g, y, slice(quarter, half))[...]
        r1b[g] = (r1b[g].astype(f32) + mine.astype(f32)).astype(rc.dtype)
        send("2b", s, r1b.at[g, :, at((1 - x) * eighth, eighth)], r2b.at[g], over_x)

    def sum_second(s):
        g = line_of(s)
        arrive("2a", s)
        sum_a = r2a[g].astype(f32) + block(r1a, g, y)[...].astype(f32)
        arrive("2b", s)
        sum_b = r2b[g].astype(f32) + r1b[g, :, at(x * eighth, eighth)].astype(f32)
        if s == lines - 1:
            return sum_a, sum_b
        s3[s, :, :eighth] = sum_a.astype(s3.dtype)
        s3[s, :, eighth:] = sum_b.astype(s3.dtype)
        send("3", s, s3.at[s], r3.at[s], over_z(g))

    for load in loads[:2]:
        load.wait()
    for s in range(lines):
        multiply(s)
        if s >= 1:
            sum_core(s - 1)
        if s >= 2:
            sum_first(s - 2)
        if s >= 3:
            sum_second(s - 3)
    sum_core(lines - 1)
    for s in range(max(lines - 2, 0), lines):
        sum_first(s)
    for s in range(max(lines - 3, 0), lines):
        own = sum_second(s)

    col_a = at(core * half + x * eighth, eighth)
    col_b = at(core * half + quarter + x * eighth, eighth)
    for s in range(lines - 1):
        arrive("3", s)
    for n, col in enumerate((col_a, col_b)):
        total = own[n]
        for s in range(lines - 1):
            total = total + r3[s, :, n * eighth : (n + 1) * eighth].astype(f32)
        outer_grad = total * 0.25
        momentum = outer_beta * mom[:, col] + outer_grad
        fresh[:, col] = momentum.astype(fresh.dtype)
        params = glob[:, col] - outer_rate * (outer_grad + outer_beta * momentum)
        block(weights, z, y, col)[...] = params.astype(weights.dtype)

    def swap(kind, step, ref, peer):
        send(kind, step, ref, ref, peer)

    def from_line(step):
        return lax.rem(z + lines - step, lines)

    for t in range(1, lines):
        peer = over_z(lax.rem(z + t, lines))
        swap("g3a", t, block(weights, z, y, col_a), peer)
        swap("g3b", t, block(weights, z, y, col_b), peer)

    def gather_third(t):
        g = from_line(t)
        if t:
            arrive("g3a", t)
        swap("g2a", t, block(weights, g, y, col_a), over_y)
        if t:
            arrive("g3b", t)
        swap("g2b", t, block(weights, g, y, col_b), over_x)
        if not t:
            swap("ma", 0, fresh.at[:, col_a], over_x)
            swap("mb", 0, fresh.at[:, col_b], over_x)

    def gather_second(t):
        g = from_line(t)
        arrive("g2a", t)
        swap("g1a", t, pair(weights, g, col_a), over_x)
        arrive("g2b", t)
        swap("g1b", t, block(weights, g, y, at(core * half + quarter, quarter)), over_y)

    def gather_first(t):
        g = from_line(t)
        arrive("g1a", t)
        arrive("g1b", t)
        swap("gc", t, pair(weights, g, at(core * half, half)), over_core)

    def project(t):
        g = from_line(t)
        arrive("gc", t)
        if not inside:
            return
        left = nxt[:, at(g * 2 * rows, 2 * rows)]
        for n in range(2):
            col = slice(n * half, (n + 1) * half)
            result = jnp.dot(left, weights[g, :, col], preferred_element_type=f32)
            total_ref[:, col] = result if not t else total_ref[:, col] + result

    if inside:
        loads[2].wait()
    for tick in range(lines + 3):
        if tick < lines:
            gather_third(tick)
        if 0 <= tick - 1 < lines:
            gather_second(tick - 1)
        if 0 <= tick - 2 < lines:
            gather_first(tick - 2)
        if tick == 2:
            arrive("ma", 0)
            arrive("mb", 0)
            swap("mc", 0, fresh.at[:, at(core * half, half)], over_core)
        if 0 <= tick - 3:
            project(tick - 3)
    arrive("mc", 0)
    if inside:
        own_out[...] = block(weights, z, y)[...]
        proj[...] = total_ref[...].astype(proj.dtype)
    for copy in copies.values():
        copy.wait_send()


def outer_step(layer_inputs, key_grad, next_inputs, global_params, own_params, momentum):
    tokens, depth = layer_inputs.shape
    rows, cols = global_params.shape
    lines = depth // (2 * rows)
    inside = (2 * rows) % 128 == 0
    low, f32 = jnp.bfloat16, jnp.float32
    half, quarter, eighth = cols // 2, cols // 4, cols // 8
    count = lines * 5 + lines - 1 + 2 * (lines - 1) + lines * 5 + 3
    both = (lines, 2 * rows) if inside else (lines, 2, rows)
    vmem = pl.BlockSpec(memory_space=pltpu.VMEM)
    hbm = pl.BlockSpec(memory_space=pl.ANY)
    shared = [
        pltpu.SemaphoreType.DMA((3,)),
        pltpu.VMEM((rows, cols), f32),
        pltpu.VMEM((rows, cols), f32),
        pltpu.VMEM((*both, half), low),
        pltpu.VMEM((*both, eighth), low),
        pltpu.VMEM((lines, rows, quarter), low),
        pltpu.VMEM((lines, rows, eighth), low),
        pltpu.VMEM((lines, rows, eighth), low),
        pltpu.VMEM((lines - 1, rows, quarter), low),
        pltpu.VMEM((lines - 1, rows, quarter), low),
        pltpu.SemaphoreType.DMA((count,)),
        pltpu.SemaphoreType.DMA((count,)),
    ]
    params = pltpu.CompilerParams(
        collective_id=0, has_side_effects=True, vmem_limit_bytes=62 * 2**20
    )
    block = jax.ShapeDtypeStruct((rows, cols), low)
    kernel = functools.partial(outer_kernel, inside)
    if inside:
        fresh, own, projected = pl.pallas_call(
            kernel,
            out_shape=(block, block, jax.ShapeDtypeStruct((tokens, cols), low)),
            in_specs=[vmem] * 3 + [hbm] * 3,
            out_specs=(vmem,) * 3,
            scratch_shapes=[
                pltpu.VMEM((*both, cols), low),
                pltpu.VMEM((*both, cols), low),
                pltpu.VMEM((tokens, depth), low),
                pltpu.VMEM((tokens, cols), f32),
                *shared,
            ],
            compiler_params=params,
        )(layer_inputs, key_grad, own_params, next_inputs, global_params, momentum)
        return own.astype(f32), fresh.astype(f32), projected
    start = lax.axis_index("fsdp") * rows
    partial = inner_rate * lax.dot_general(
        layer_inputs, key_grad, (((0,), (0,)), ((), ())), preferred_element_type=f32
    )
    mine = lax.dynamic_slice_in_dim(partial, start, rows, 0) + (global_params - own_params)
    partial = lax.dynamic_update_slice_in_dim(partial, mine, start, 0).astype(low)
    fresh, weights = pl.pallas_call(
        kernel,
        out_shape=(block, jax.ShapeDtypeStruct((*both, cols), low)),
        in_specs=[vmem] + [hbm] * 2,
        out_specs=(vmem,) * 2,
        scratch_shapes=shared,
        compiler_params=params,
    )(partial.reshape(*both, cols), global_params, momentum)
    weights = weights.reshape(depth, cols)
    projected = jnp.dot(next_inputs, weights, preferred_element_type=f32)
    own = lax.dynamic_slice_in_dim(weights, start, rows, 0)
    return own.astype(f32), fresh.astype(f32), projected.astype(low)


def body(
    layer_inputs,
    queries,
    saved_keys,
    saved_values,
    out_grad,
    global_params,
    replica_params,
    outer_momentum,
    next_inputs,
):
    key_grad = attention_keys(queries, saved_keys, saved_values, out_grad)
    return outer_step(
        layer_inputs, key_grad, next_inputs, global_params, replica_params[0], outer_momentum
    )


def solution(mesh):
    return jax.shard_map(
        body,
        mesh=mesh,
        in_specs=(
            P(("rep", "fsdp"), None),
            P(("rep", "fsdp"), None),
            P(("rep", "fsdp"), None),
            P(("rep", "fsdp"), None),
            P(("rep", "fsdp"), None),
            P("fsdp", None),
            P("rep", "fsdp", None),
            P("fsdp", None),
            P(("rep", "fsdp"), None),
        ),
        out_specs=(P("fsdp", None), P("fsdp", None), P(("rep", "fsdp"), None)),
        check_vma=False,
    )
```

time: 204 us -> 144 us (0.71)
  the two profiles are of different devices: /device:TPU:0 before, /device:TPU:17 now
where the time goes in v2:
time: 144 us; the launch traced here: 143 us
  Pallas kernels  137 us (95%)
  other arithmetic  4.74 us (3%)
    pallas_call x1, Pallas kernels, outer_step(): pl.pallas_call(kernel, out_shape=(block, block, jax.ShapeDtypeStruct((tok...  128 us
    pallas_call x1, Pallas kernels, attention_keys(): pl.pallas_call(attention_kernel, grid=(KVH,), out_shape=jax.ShapeDtypeStr...  9.3 us
    convert_element_type x2, other arithmetic, outer_step(): return (own.astype(f32), fresh.astype(f32), projected)  4.74 us

profile of v2, /device:TPU:17, one launch (start us, length us, event | category | flops | bytes accessed | tf_op | source)
XLA Modules:
  0.0 143.3 jit_solution(9420799587727771697)
XLA Ops:
  0.6 9.3 %shard_map.130.refs_1_ = bf16[256,1024]{1,0:T(8,128)(2,1)} custom-call(bf16[256,2048]{1,0:T(8,128)(2,1)} %q_ref.1, bf16[256,1024]{1,0:T(8,128)(2,1)} %k_ref.1, bf16[256,1024]{1,0:T(8,128)(2,1)} %v_ref.1, bf16[256,2048]{1,0:T(8,128)(2,1)} %g_ref.1, f32[256,128]{1,0:T(8,128)} %constant.4.clone.cos_ref, f32[256,128]{1,0:T(8,128)} %constant.5.clone.sin_ref), custom_call_target="tpu_custom_call" | custom-call | tf_op jit(solution)/shard_map/pallas_call | solution.py:66
  9.9 127.8 %shard_map.131 = (bf16[576,1024]{1,0:T(8,128)(2,1)}, bf16[576,1024]{1,0:T(8,128)(2,1)}, bf16[256,1024]{1,0:T(8,128)(2,1)}) custom-call(bf16[256,4608]{1,0:T(8,128)(2,1)} %refs_0_.1, bf16[256,1024]{1,0:T(8,128)(2,1)} %shard_map.130.refs_1_, f32[576,1024]{1,0:T(8,128)} %bitcast.1, bf16[256,4608]{1,0:T(8,128)(2,1)} %refs_3_.1, f32[576,1024]{1,0:T(8,128)} %refs_4_.1, ...), custom_call_target="tpu_custom_call" | custom-call | tf_op jit(solution)/shard_map/pallas_call | solution.py:333
  137.7 0.0 copy-start
  137.7 3.1 %convert_element_type.6 = f32[576,1024]{1,0:T(8,128)} convert(bf16[576,1024]{1,0:T(8,128)(2,1)} %get-tuple-element.6) | non-fusion elementwise | flops 589824 | bytes 3538944 | tf_op jit(solution)/shard_map/convert_element_type | solution.py:347
  140.8 0.0 copy-done
  140.8 0.0 copy-start.1
  140.8 1.7 %convert_element_type.7 = f32[576,1024]{1,0:T(8,128)} convert(bf16[576,1024]{1,0:T(8,128)(2,1)S(1)} %copy-done) | non-fusion elementwise | flops 589824 | bytes 3538944 | tf_op jit(solution)/shard_map/convert_element_type | solution.py:347
  142.5 0.0 copy-done.1
  142.5 0.8 copy.15
Async XLA Ops:
  137.7 3.1 %copy-start = (bf16[576,1024]{1,0:T(8,128)(2,1)S(1)}, bf16[576,1024]{1,0:T(8,128)(2,1)}, u32[]{:S(2)}) copy-start(bf16[576,1024]{1,0:T(8,128)(2,1)} %get-tuple-element.7) | copy-start | bytes 3538948
  140.8 1.7 %copy-start.1 = (bf16[256,1024]{1,0:T(8,128)(2,1)S(1)}, bf16[256,1024]{1,0:T(8,128)(2,1)}, u32[]{:S(2)}) copy-start(bf16[256,1024]{1,0:T(8,128)(2,1)} %get-tuple-element.14) | copy-start | bytes 1572868

commit v3 on v2

--- a/solution.py
+++ b/solution.py
@@ -74,8 +74,8 @@
 
 def outer_kernel(inside, *refs):
     if inside:
-        (layer, keyg, drift, nxt_in, glob_in, mom_in, fresh, own_out, proj) = refs[:9]
-        (part, weights, nxt, total_ref, load_sem, *rest) = refs[9:]
+        (keyg, layer_in, drift_in, nxt_in, glob_in, mom_in, fresh, own_out, proj) = refs[:9]
+        (part, weights, layer, drift, nxt, total_ref, load_sem, *rest) = refs[9:]
     else:
         (part, glob_in, mom_in, fresh, weights, load_sem, *rest) = refs
     glob, mom, rc, r1a, r1b, r2a, r2b, s3, r3, send_sem, recv_sem = rest
@@ -104,11 +104,21 @@
             return ref.at[g, at(yy * rows, rows), col]
         return ref.at[g, yy, :, col]
 
+    def line_of(step):
+        return lax.rem(z + 1 + step, lines)
+
+    moves = []
+    if inside:
+        for s in range(lines):
+            cols_of = at(line_of(s) * 2 * rows, 2 * rows)
+            moves.append((layer_in.at[:, cols_of], layer.at[:, cols_of]))
+        moves.append((drift_in, drift))
+    moves.append((glob_in, glob))
+    moves.append((mom_in, mom))
+    if inside:
+        moves.append((nxt_in, nxt))
     loads = [
-        pltpu.make_async_copy(src, dst, load_sem.at[n])
-        for n, (src, dst) in enumerate(
-            [(glob_in, glob), (mom_in, mom)] + ([(nxt_in, nxt)] if inside else [])
-        )
+        pltpu.make_async_copy(src, dst, load_sem.at[n]) for n, (src, dst) in enumerate(moves)
     ]
     for load in loads:
         load.start()
@@ -140,29 +150,39 @@
     def arrive(kind, step):
         copies[kind, step].wait_recv()
 
-    def line_of(step):
-        return lax.rem(z + 1 + step, lines)
-
     def multiply(s):
         g = line_of(s)
+        theirs, own_half = at((1 - core) * half, half), at(core * half, half)
         if inside:
             width = 2 * rows
             tile = 128
-
-            def one(n, carry):
-                left = layer[:, at(g * width + n * tile, tile)]
-                result = lax.dot_general(
-                    left, keyg[...], (((0,), (0,)), ((), ())), preferred_element_type=f32
-                )
-                part[g, at(n * tile, tile), :] = (result * inner_rate).astype(part.dtype)
-                return carry
-
-            lax.fori_loop(0, width // tile, one, 0)
+            loads[s].wait()
             if s == lines - 1:
-                mine = block(part, g, y)
-                mine[...] = (mine[...].astype(f32) + (glob[...] - drift[...])).astype(part.dtype)
-        theirs = at((1 - core) * half, half)
+                for load in loads[lines : lines + 2]:
+                    load.wait()
+
+            def product(col):
+                def one(n, carry):
+                    left = layer[:, at(g * width + n * tile, tile)]
+                    result = lax.dot_general(
+                        left,
+                        keyg[:, col],
+                        (((0,), (0,)), ((), ())),
+                        preferred_element_type=f32,
+                    )
+                    part[g, at(n * tile, tile), col] = (result * inner_rate).astype(part.dtype)
+                    return carry
+
+                lax.fori_loop(0, width // tile, one, 0)
+                if s == lines - 1:
+                    mine = block(part, g, y, col)
+                    moved = glob[:, col] - drift[:, col]
+                    mine[...] = (mine[...].astype(f32) + moved).astype(part.dtype)
+
+            product(theirs)
         send("c", s, pair(part, g, theirs), pair(rc, g), over_core)
+        if inside:
+            product(own_half)
 
     def sum_core(s):
         g = line_of(s)
@@ -199,22 +219,21 @@
         s3[s, :, eighth:] = sum_b.astype(s3.dtype)
         send("3", s, s3.at[s], r3.at[s], over_z(g))
 
-    for load in loads[:2]:
+    multiply(0)
+    sum_core(0)
+    for s in range(1, lines):
+        multiply(s)
+        sum_core(s)
+        sum_first(s - 1)
+        if s >= 2:
+            sum_second(s - 2)
+    sum_first(lines - 1)
+    if lines > 1:
+        sum_second(lines - 2)
+    own = sum_second(lines - 1)
+
+    for load in loads[lines + 2 :] if inside else loads:
         load.wait()
-    for s in range(lines):
-        multiply(s)
-        if s >= 1:
-            sum_core(s - 1)
-        if s >= 2:
-            sum_first(s - 2)
-        if s >= 3:
-            sum_second(s - 3)
-    sum_core(lines - 1)
-    for s in range(max(lines - 2, 0), lines):
-        sum_first(s)
-    for s in range(max(lines - 3, 0), lines):
-        own = sum_second(s)
-
     col_a = at(core * half + x * eighth, eighth)
     col_b = at(core * half + quarter + x * eighth, eighth)
     for s in range(lines - 1):
@@ -248,9 +267,6 @@
         if t:
             arrive("g3b", t)
         swap("g2b", t, block(weights, g, y, col_b), over_x)
-        if not t:
-            swap("ma", 0, fresh.at[:, col_a], over_x)
-            swap("mb", 0, fresh.at[:, col_b], over_x)
 
     def gather_second(t):
         g = from_line(t)
@@ -276,22 +292,30 @@
             result = jnp.dot(left, weights[g, :, col], preferred_element_type=f32)
             total_ref[:, col] = result if not t else total_ref[:, col] + result
 
-    if inside:
-        loads[2].wait()
-    for tick in range(lines + 3):
-        if tick < lines:
-            gather_third(tick)
-        if 0 <= tick - 1 < lines:
-            gather_second(tick - 1)
-        if 0 <= tick - 2 < lines:
-            gather_first(tick - 2)
-        if tick == 2:
+    gather_third(0)
+    gather_second(0)
+    if lines > 1:
+        gather_third(1)
+    swap("ma", 0, fresh.at[:, col_a], over_x)
+    swap("mb", 0, fresh.at[:, col_b], over_x)
+    for t in range(1, lines):
+        if t == 1:
+            gather_first(0)
+        gather_second(t)
+        if t + 1 < lines:
+            gather_third(t + 1)
+        if t > 1:
+            gather_first(t - 1)
+            project(t - 2)
+        else:
             arrive("ma", 0)
             arrive("mb", 0)
             swap("mc", 0, fresh.at[:, at(core * half, half)], over_core)
-        if 0 <= tick - 3:
-            project(tick - 3)
+    gather_first(lines - 1)
+    if lines > 1:
+        project(lines - 2)
     arrive("mc", 0)
+    project(lines - 1)
     if inside:
         own_out[...] = block(weights, z, y)[...]
         proj[...] = total_ref[...].astype(proj.dtype)
@@ -311,7 +335,7 @@
     vmem = pl.BlockSpec(memory_space=pltpu.VMEM)
     hbm = pl.BlockSpec(memory_space=pl.ANY)
     shared = [
-        pltpu.SemaphoreType.DMA((3,)),
+        pltpu.SemaphoreType.DMA((lines + 4,)),
         pltpu.VMEM((rows, cols), f32),
         pltpu.VMEM((rows, cols), f32),
         pltpu.VMEM((*both, half), low),
@@ -333,17 +357,19 @@
         fresh, own, projected = pl.pallas_call(
             kernel,
             out_shape=(block, block, jax.ShapeDtypeStruct((tokens, cols), low)),
-            in_specs=[vmem] * 3 + [hbm] * 3,
+            in_specs=[vmem] + [hbm] * 5,
             out_specs=(vmem,) * 3,
             scratch_shapes=[
                 pltpu.VMEM((*both, cols), low),
                 pltpu.VMEM((*both, cols), low),
                 pltpu.VMEM((tokens, depth), low),
+                pltpu.VMEM((rows, cols), f32),
+                pltpu.VMEM((tokens, depth), low),
                 pltpu.VMEM((tokens, cols), f32),
                 *shared,
             ],
             compiler_params=params,
-        )(layer_inputs, key_grad, own_params, next_inputs, global_params, momentum)
+        )(key_grad, layer_inputs, own_params, next_inputs, global_params, momentum)
         return own.astype(f32), fresh.astype(f32), projected
     start = lax.axis_index("fsdp") * rows
     partial = inner_rate * lax.dot_general(

time: 144 us -> 131 us (0.910)
  the two profiles are of different devices: /device:TPU:17 before, /device:TPU:0 now
where the time goes in v3:
time: 131 us; the launch traced here: 129 us
  Pallas kernels  123 us (94%)
  other arithmetic  4.74 us (4%)
    pallas_call x1, Pallas kernels, outer_step(): pl.pallas_call(kernel, out_shape=(block, block, jax.ShapeDtypeStruct((tok...  114 us
    pallas_call x1, Pallas kernels, attention_keys(): pl.pallas_call(attention_kernel, grid=(KVH,), out_shape=jax.ShapeDtypeStr...  9.31 us
    convert_element_type x2, other arithmetic, outer_step(): return (own.astype(f32), fresh.astype(f32), projected)  4.74 us

profile of v3, /device:TPU:0, one launch (start us, length us, event | category | flops | bytes accessed | tf_op | source)
XLA Modules:
  0.0 129.5 jit_solution(17241583894817650345)
XLA Ops:
  0.6 9.3 %shard_map.130.refs_0_ = bf16[256,1024]{1,0:T(8,128)(2,1)} custom-call(bf16[256,2048]{1,0:T(8,128)(2,1)} %q_ref.1, bf16[256,1024]{1,0:T(8,128)(2,1)} %k_ref.1, bf16[256,1024]{1,0:T(8,128)(2,1)} %v_ref.1, bf16[256,2048]{1,0:T(8,128)(2,1)} %g_ref.1, f32[256,128]{1,0:T(8,128)} %constant.4.clone.cos_ref, f32[256,128]{1,0:T(8,128)} %constant.5.clone.sin_ref), custom_call_target="tpu_custom_call" | custom-call | tf_op jit(solution)/shard_map/pallas_call | solution.py:66
  9.9 113.9 %shard_map.131 = (bf16[576,1024]{1,0:T(8,128)(2,1)}, bf16[576,1024]{1,0:T(8,128)(2,1)}, bf16[256,1024]{1,0:T(8,128)(2,1)}) custom-call(bf16[256,1024]{1,0:T(8,128)(2,1)} %shard_map.130.refs_0_, bf16[256,4608]{1,0:T(8,128)(2,1)} %refs_1_.1, f32[576,1024]{1,0:T(8,128)} %bitcast.1, bf16[256,4608]{1,0:T(8,128)(2,1)} %refs_3_.1, f32[576,1024]{1,0:T(8,128)} %refs_4_.1, ...), custom_call_target="tpu_custom_call" | custom-call | tf_op jit(solution)/shard_map/pallas_call | solution.py:357
  123.9 0.0 copy-start
  123.9 3.1 %convert_element_type.6 = f32[576,1024]{1,0:T(8,128)} convert(bf16[576,1024]{1,0:T(8,128)(2,1)} %get-tuple-element.6) | non-fusion elementwise | flops 589824 | bytes 3538944 | tf_op jit(solution)/shard_map/convert_element_type | solution.py:373
  127.0 0.0 copy-done
  127.0 0.0 copy-start.1
  127.0 1.7 %convert_element_type.7 = f32[576,1024]{1,0:T(8,128)} convert(bf16[576,1024]{1,0:T(8,128)(2,1)S(1)} %copy-done) | non-fusion elementwise | flops 589824 | bytes 3538944 | tf_op jit(solution)/shard_map/convert_element_type | solution.py:373
  128.7 0.0 copy-done.1
  128.7 0.8 copy.15
Async XLA Ops:
  123.9 3.1 %copy-start = (bf16[576,1024]{1,0:T(8,128)(2,1)S(1)}, bf16[576,1024]{1,0:T(8,128)(2,1)}, u32[]{:S(2)}) copy-start(bf16[576,1024]{1,0:T(8,128)(2,1)} %get-tuple-element.7) | copy-start | bytes 3538948
  127.0 1.7 %copy-start.1 = (bf16[256,1024]{1,0:T(8,128)(2,1)S(1)}, bf16[256,1024]{1,0:T(8,128)(2,1)}, u32[]{:S(2)}) copy-start(bf16[256,1024]{1,0:T(8,128)(2,1)} %get-tuple-element.14) | copy-start | bytes 1572868
